TPU v7x, 128 devices: a whole 4x4x4 slice. The times are simulated.
128 devices in a mesh: gx: 4 (over y), gy: 32 (over x, z, core).
Axes of the slice: x: 4, y: 4, z: 4, core: 2. Of those that a mesh axis runs over, the one named last changes fastest.
Arguments:
- vertex_state: bfloat16 [1024, 256, 128], P(('gx', 'gy')), may hold values from -6 to 6
- edge_state: bfloat16 [1024, 1536, 128], P(('gx', 'gy')), may hold values from -6 to 6
- senders: int32 [1024, 1536], P(('gx', 'gy')), may hold values from 0 to 511
- receivers: int32 [1024, 1536], P(('gx', 'gy')), may hold values from 0 to 255
- counts: int32 [1024], P(('gx', 'gy')), may hold values from 768 to 1536
- border_rows: int32 [1024, 2, 128], P(('gx', 'gy')), may hold values from 0 to 255
- old_neighbours: int32 [1024, 2], P(('gx', 'gy')), may hold values from 0 to 1023, as said below
- new_neighbours: int32 [1024, 2], P(('gx', 'gy')), may hold values from 0 to 1023, as said below
- new_place: int32 [1024], P(('gx', 'gy')), may hold values from 0 to 1023, as said below
- weights_in: bfloat16 [3, 5, 128, 128], replicated, may hold values from -0.5 to 0.5
- weights_out: bfloat16 [3, 2, 128, 128], replicated, may hold values from -0.5 to 0.5
- biases: float32 [3, 6, 128], replicated, may hold values from -3 to 3
- norm_gains: float32 [3, 2, 128], replicated, may hold values from 0.25 to 1.75
Outputs:
- vertex_out: bfloat16 [1024, 256, 128], P(('gx', 'gy'))
- edge_out: bfloat16 [1024, 1536, 128], P(('gx', 'gy'))
Inputs may be any that keep to these rules, and one draw needn't show every extreme that they name: A permutation of the patches. With devices numbered gx-index times the size of gy plus gy-index, patch p stands on device p // 8 and moves to device new_place[p] // 8, which has the same gx-index; one device sends at most 1 patch to any one device, and some pair of devices reaches 1. old_neighbours[p, 0] stands on the device whose gy-index is one less than that of p's device (cyclically) and whose gx-index is the same; old_neighbours[p, 1] on the device whose gx-index is one less (cyclically) and whose gy-index is the same. new_neighbours[new_place[p], k] = new_place[old_neighbours[p, k]]; in the new positions it follows the same rule as old_neighbours.
All inputs are finite; a program needn't handle non-finite values.
Results may differ from a plain program's by a relative error of at most 0.0066.
Values may be sent and summed in bfloat16 or wider, within the bound.
No kernel may reach another device: no remote copies, remote signals or barrier semaphores. Data moves between devices by JAX's collectives and lax.ppermute only.
A program may use at most 128 MiB of HBM per device.

v0:
```python
import jax
import jax.numpy as jnp
from jax import lax
from jax.sharding import PartitionSpec as P

STEPS_OLD = 2


def shifted(shard, axis, by):
    devices = lax.axis_size(axis)
    return lax.ppermute(shard, axis, [(i, (i + by) % devices) for i in range(devices)])


def product(left, right):
    return jnp.dot(left, right, preferred_element_type=jnp.float32)


def normalize(values, scale_row, shift_row):
    center = values - jnp.mean(values, axis=-1, keepdims=True)
    spread = jnp.mean(center * center, axis=-1, keepdims=True)
    return center * lax.rsqrt(spread + 1e-05) * scale_row + shift_row


def picker(indices, offset, number):
    columns = offset + jnp.arange(number, dtype=jnp.int32)
    return (indices[:, None] == columns[None, :]).astype(jnp.bfloat16)


def fetch_ghosts(vertex_state, border_rows, neighbour_slots):
    patch_rows = jnp.arange(vertex_state.shape[0], dtype=jnp.int32)[:, None]
    along_gy = vertex_state[patch_rows, border_rows[:, 0]]
    along_gx = vertex_state[patch_rows, border_rows[:, 1]]
    came_gy = shifted(along_gy, "gy", 1)
    came_gx = shifted(along_gx, "gx", 1)
    return jnp.concatenate([came_gy[neighbour_slots[:, 0]], came_gx[neighbour_slots[:, 1]]], axis=1)


def edge_start(layer_weights, pieces):
    weights_in, weights_out, bias_rows, gain_rows = layer_weights
    vertex_block, edge_block, sender_ids, receiver_ids = pieces
    vertex_count = vertex_block.shape[0]
    receiver_terms = product(vertex_block, weights_in[2]).astype(jnp.bfloat16)
    started = product(edge_block, weights_in[0]) + product(
        picker(receiver_ids, 0, vertex_count), receiver_terms
    )
    started = started + bias_rows[0]
    own_terms = product(vertex_block, weights_in[1]).astype(jnp.bfloat16)
    started = started + product(picker(sender_ids, 0, vertex_count), own_terms)
    return started


def patch_finish(layer_weights, pieces):
    weights_in, weights_out, bias_rows, gain_rows = layer_weights
    vertex_block, ghost_block, edge_block, sender_ids, receiver_ids, edge_count, started = pieces
    vertex_count = vertex_block.shape[0]
    ghost_count = ghost_block.shape[0]
    edge_total = edge_block.shape[0]
    ghost_terms = product(ghost_block, weights_in[1]).astype(jnp.bfloat16)
    summed = started + product(picker(sender_ids, vertex_count, ghost_count), ghost_terms)
    edge_hidden = jax.nn.relu(summed).astype(jnp.bfloat16)
    edge_update = normalize(
        product(edge_hidden, weights_out[0]) + bias_rows[1], gain_rows[0], bias_rows[2]
    )
    live = jnp.arange(edge_total, dtype=jnp.int32) < edge_count
    widened = edge_block.astype(jnp.float32)
    fresh_edges = jnp.where(live[:, None], widened + edge_update, widened).astype(jnp.bfloat16)
    vertex_ids = jnp.arange(vertex_count, dtype=jnp.int32)
    incoming = ((vertex_ids[:, None] == receiver_ids[None, :]) & live[None, :]).astype(jnp.bfloat16)
    aggregate = product(incoming, fresh_edges).astype(jnp.bfloat16)
    node_hidden = (
        product(vertex_block, weights_in[3]) + product(aggregate, weights_in[4]) + bias_rows[3]
    )
    node_hidden = jax.nn.relu(node_hidden).astype(jnp.bfloat16)
    vertex_update = normalize(
        product(node_hidden, weights_out[1]) + bias_rows[4], gain_rows[1], bias_rows[5]
    )
    fresh_vertices = (vertex_block.astype(jnp.float32) + vertex_update).astype(jnp.bfloat16)
    return (fresh_vertices, fresh_edges)


def run_step(layer_weights, vertex_state, edge_state, senders, receivers, counts, ghosts):
    started = lax.map(
        lambda pieces: edge_start(layer_weights, pieces),
        (vertex_state, edge_state, senders, receivers),
    )
    return lax.map(
        lambda pieces: patch_finish(layer_weights, pieces),
        (vertex_state, ghosts, edge_state, senders, receivers, counts, started),
    )


def local(
    vertex_state,
    edge_state,
    senders,
    receivers,
    counts,
    border_rows,
    old_neighbours,
    new_neighbours,
    new_place,
    weights_in,
    weights_out,
    biases,
    norm_gains,
):
    patch_count = vertex_state.shape[0]
    edge_total = edge_state.shape[1]

    def weights_of(step_index):
        return (
            weights_in[step_index],
            weights_out[step_index],
            biases[step_index],
            norm_gains[step_index],
        )

    neighbour_slots = old_neighbours % patch_count
    for step_index in range(STEPS_OLD):
        ghosts = fetch_ghosts(vertex_state, border_rows, neighbour_slots)
        vertex_state, edge_state = run_step(
            weights_of(step_index), vertex_state, edge_state, senders, receivers, counts, ghosts
        )
    cycle_size = lax.axis_size("gy")
    capacity = (patch_count + cycle_size - 1) // cycle_size
    target = new_place // patch_count
    target_gy = target % cycle_size
    target_slot = new_place % patch_count
    positions = jnp.arange(patch_count, dtype=jnp.int32)
    earlier = (target_gy[:, None] == target_gy[None, :]) & (positions[:, None] > positions[None, :])
    before = jnp.sum(earlier.astype(jnp.int32), axis=1)
    place_index = target_gy * capacity + before
    outbox = cycle_size * capacity
    outbox_ids = jnp.arange(outbox, dtype=jnp.int32)
    filled = place_index[None, :] == outbox_ids[:, None]
    source = jnp.sum(jnp.where(filled, positions[None, :], 0), axis=1)
    occupied = jnp.any(filled, axis=1)
    id_rows = jnp.concatenate([senders, receivers, border_rows.reshape(patch_count, -1)], axis=1)[
        source
    ]
    header = jnp.stack([jnp.where(occupied, target_slot[source], -1), counts[source]], axis=1)
    arrived = (
        lax.all_to_all(vertex_state[source], "gy", split_axis=0, concat_axis=0, tiled=True),
        lax.all_to_all(edge_state[source], "gy", split_axis=0, concat_axis=0, tiled=True),
        lax.all_to_all(id_rows, "gy", split_axis=0, concat_axis=0, tiled=True),
        lax.all_to_all(header, "gy", split_axis=0, concat_axis=0, tiled=True),
    )
    landing = arrived[3][:, 0]
    chosen = jnp.sum(
        jnp.where(landing[None, :] == positions[:, None], outbox_ids[None, :], 0), axis=1
    )
    vertex_state = arrived[0][chosen]
    edge_state = arrived[1][chosen]
    id_rows = arrived[2][chosen]
    counts = arrived[3][chosen, 1]
    senders = id_rows[:, :edge_total]
    receivers = id_rows[:, edge_total : 2 * edge_total]
    border_rows = id_rows[:, 2 * edge_total :].reshape(patch_count, 2, -1)
    neighbour_slots = new_neighbours % patch_count
    step_index = 0
    ghosts = fetch_ghosts(vertex_state, border_rows, neighbour_slots)
    vertex_state, edge_state = run_step(
        weights_of(STEPS_OLD + step_index),
        vertex_state,
        edge_state,
        senders,
        receivers,
        counts,
        ghosts,
    )
    return (vertex_state, edge_state)


def solution(mesh):
    placed = (
        P(("gx", "gy"), None, None),
        P(("gx", "gy"), None, None),
        P(("gx", "gy"), None),
        P(("gx", "gy"), None),
        P(("gx", "gy")),
        P(("gx", "gy"), None, None),
        P(("gx", "gy"), None),
        P(("gx", "gy"), None),
        P(("gx", "gy")),
        P(),
        P(),
        P(),
        P(),
    )
    return jax.shard_map(
        local,
        mesh=mesh,
        in_specs=placed,
        out_specs=(P(("gx", "gy"), None, None), P(("gx", "gy"), None, None)),
        check_vma=False,
    )
```

profile of v0, /device:TPU:36, one launch (start us, length us, event | category | flops | bytes accessed | tf_op | source)
XLA Modules:
  0.0 611.8 jit_solution(4008054103573757114)
XLA Ops:
  1.5 17.9 %gather_fusion = bf16[1024,128]{1,0:T(8,128)(2,1)} fusion(bf16[8,256,128]{2,1,0:T(8,128)(2,1)} %param.25, s32[1024]{0:T(1024)S(1)} %fusion.237), kind=kCustom, calls=%fused_computation | custom fusion | bytes 532480 | tf_op jit(solution)/shard_map/gather | solution.py:31
  19.4 10.5 %gather_fusion.2 = bf16[1024,128]{1,0:T(8,128)(2,1)} fusion(bf16[8,256,128]{2,1,0:T(8,128)(2,1)S(1)} %copy-done.2, s32[1024]{0:T(1024)S(1)} %fusion.241), kind=kCustom, calls=%fused_computation.2 | custom fusion | bytes 532480 | tf_op jit(solution)/shard_map/gather | solution.py:32
  34.1 8.9 %all-to-all-start.1 = ((s32[32,1,2]{2,1,0:T(1,128)}), s32[32,1,2]{2,1,0:T(1,128)S(1)}, u32[]{:S(2)}, u32[]{:S(2)}) async-start(s32[32,1,2]{2,1,0:T(1,128)} %copy.72), calls=%async_computation.1 | async-start | bytes 32768 | tf_op jit(solution)/shard_map/all_to_all | solution.py:146
  43.1 3.2 broadcast.355.clone
  46.3 26.2 %while.66 = (s32[]{:T(128)}, f32[8,1536,128]{2,1,0:T(8,128)}, bf16[8,1536,128]{2,1,0:T(8,128)(2,1)}, bf16[5,128,128]{2,1,0:T(8,128)(2,1)S(1)}, s32[8,1536]{1,0:T...) while((s32[]{:T(128)}, f32[8,1536,128]{2,1,0:T(8,128)}, ...), condition=%wide.region_1.2_spmd, body=%wide.region_0.1_spmd.sunk | while | flops 269877248 | bytes 4598885 | solution.py:82
  80.4 62.8 %while.67 = (s32[]{:T(128)}, bf16[8,256,128]{1,2,0:T(8,128)(2,1)S(1)}, bf16[8,1536,128]{1,2,0:T(8,128)(2,1)}, bf16[8,256,128]{2,1,0:T(8,128)(2,1)S(1)}, bf16[5,1...) while((s32[]{:T(128)}, ...), condition=%wide.region_7.8_spmd, body=%wide.region_2.7_spmd.sunk | while | flops 290131456 | bytes 8022189 | solution.py:86
  143.5 10.5 %gather_fusion.4 = bf16[1024,128]{1,0:T(8,128)(2,1)} fusion(bf16[8,256,128]{2,1,0:T(8,128)(2,1)S(1)} %copy.68, s32[1024]{0:T(1024)S(1)} %fusion.237), kind=kCustom, calls=%fused_computation.4 | custom fusion | bytes 532480 | tf_op jit(solution)/shard_map/gather | solution.py:31
  154.1 10.5 %gather_fusion.6 = bf16[1024,128]{1,0:T(8,128)(2,1)} fusion(bf16[8,256,128]{2,1,0:T(8,128)(2,1)S(1)} %copy.68, s32[1024]{0:T(1024)S(1)} %fusion.241), kind=kCustom, calls=%fused_computation.6 | custom fusion | bytes 532480 | tf_op jit(solution)/shard_map/gather | solution.py:32
  166.3 3.2 broadcast.355.clone.1
  169.5 26.6 %while.68 = (s32[]{:T(128)}, f32[8,1536,128]{2,1,0:T(8,128)}, bf16[8,1536,128]{1,2,0:T(8,128)(2,1)}, bf16[5,128,128]{2,1,0:T(8,128)(2,1)S(1)}, s32[8,1536]{1,0:T...) while((s32[]{:T(128)}, f32[8,1536,128]{2,1,0:T(8,128)}, ...), condition=%wide.region_9.10_spmd, body=%wide.region_8.9_spmd.sunk | while | flops 269877248 | bytes 4598885 | solution.py:82
  200.0 8.0 %all-to-all-start.2 = ((s32[32,1,3328]{2,1,0:T(1,128)}), s32[32,1,3328]{2,1,0:T(1,128)}, u32[]{:S(2)}, u32[]{:S(2)}) async-start(s32[32,1,3328]{2,1,0:T(1,128)} %copy.74), calls=%async_computation.2 | async-start | bytes 851968 | tf_op jit(solution)/shard_map/all_to_all | solution.py:145
  210.0 61.6 %while.69 = (s32[]{:T(128)}, bf16[8,256,128]{2,1,0:T(8,128)(2,1)S(1)}, bf16[8,1536,128]{1,2,0:T(8,128)(2,1)}, bf16[8,256,128]{1,2,0:T(8,128)(2,1)S(1)}, bf16[5,1...) while((s32[]{:T(128)}, ...), condition=%wide.region_15.16_spmd, body=%wide.region_10.15_spmd.sunk | while | flops 290131456 | bytes 6449325 | solution.py:86
  214.3 2.1 bitcast_dynamic-update-slice_fusion.5
  229.7 2.1 bitcast_dynamic-update-slice_fusion.5
  237.4 2.1 bitcast_dynamic-update-slice_fusion.5
  245.1 2.1 bitcast_dynamic-update-slice_fusion.5
  252.8 2.1 bitcast_dynamic-update-slice_fusion.5
  260.5 2.1 bitcast_dynamic-update-slice_fusion.5
  271.6 2.2 gather_fusion.8
  273.7 7.7 %all-to-all-start = ((bf16[32,256,128]{2,1,0:T(8,128)(2,1)}), bf16[32,256,128]{2,1,0:T(8,128)(2,1)}, u32[]{:S(2)}, u32[]{:S(2)}) async-start(bf16[32,256,128]{2,1,0:T(8,128)(2,1)} %gather_fusion.8), calls=%async_computation | async-start | bytes 4194304 | tf_op jit(solution)/shard_map/all_to_all | solution.py:143
  281.5 6.4 %gather_fusion.15 = bf16[32,1536,128]{1,2,0:T(8,128)(2,1)} fusion(bf16[8,1536,128]{1,2,0:T(8,128)(2,1)S(1)} %copy-done.1, s32[1024]{0:T(1024)S(1)} %pad_clamp_fusion.3), kind=kCustom, calls=%fused_computation.15 | custom fusion | bytes 25165952 | tf_op jit(solution)/shard_map/gather | solution.py:144
  287.8 18.0 %all-to-all-done = bf16[32,256,128]{2,1,0:T(8,128)(2,1)} async-done(((bf16[32,256,128]{2,1,0:T(8,128)(2,1)}), bf16[32,256,128]{2,1,0:T(8,128)(2,1)}, u32[]{:S(2)}, u32[]{:S(2)}) %all-to-all-start) | async-done | bytes 2097184 | tf_op jit(solution)/shard_map/all_to_all | solution.py:143
  305.9 9.5 %all-to-all-start.3 = ((bf16[32,1536,128]{1,2,0:T(8,128)(2,1)}), bf16[32,1536,128]{1,2,0:T(8,128)(2,1)}, u32[]{:S(2)}, u32[]{:S(2)}) async-start(bf16[32,1536,128]{1,2,0:T(8,128)(2,1)} %gather_fusion.15), calls=%async_computation.3 | async-start | bytes 25165824 | tf_op jit(solution)/shard_map/all_to_all | solution.py:144
  318.0 2.2 gather_fusion.11
  320.3 5.8 gather_fusion.17
  326.3 5.8 gather_fusion.19
  333.7 103.0 %collective-permute-done.4 = bf16[8,128,128]{2,1,0:T(8,128)(2,1)S(1)} collective-permute-done((bf16[8,128,128]{2,1,0:T(8,128)(2,1)S(1)}, bf16[8,128,128]{2,1,0:T(8,128)(2,1)S(1)}, u32[]{:S(2)}, u32[]{:S(2)}) %collective-permute-start.4) | collective-permute-done | bytes 262176 | tf_op jit(solution)/shard_map/ppermute | solution.py:11
  438.0 74.7 %all-to-all-done.3 = bf16[32,1536,128]{1,2,0:T(8,128)(2,1)} async-done(((bf16[32,1536,128]{1,2,0:T(8,128)(2,1)}), bf16[32,1536,128]{1,2,0:T(8,128)(2,1)}, u32[]{:S(2)}, u32[]{:S(2)}) %all-to-all-start.3) | async-done | bytes 12582944 | tf_op jit(solution)/shard_map/all_to_all | solution.py:144
  512.7 7.0 %gather_fusion.16 = bf16[8,1536,128]{1,2,0:T(8,128)(2,1)} fusion(bf16[32,1536,128]{1,2,0:T(8,128)(2,1)} %all-to-all-done.3, s32[1024]{0:T(1024)S(1)} %pad_clamp_fusion.2), kind=kCustom, calls=%fused_computation.16 | custom fusion | bytes 6291488 | tf_op jit(solution)/shard_map/gather | solution.py:153
  519.7 3.2 broadcast.355
  522.8 26.6 %while.70 = (s32[]{:T(128)}, f32[8,1536,128]{2,1,0:T(8,128)}, bf16[8,1536,128]{1,2,0:T(8,128)(2,1)}, bf16[5,128,128]{2,1,0:T(8,128)(2,1)S(1)}, s32[8,1536]{1,0:T...) while((s32[]{:T(128)}, f32[8,1536,128]{2,1,0:T(8,128)}, ...), condition=%wide.region_21.22_spmd, body=%wide.region_20.21_spmd.sunk | while | flops 269877248 | bytes 4598885 | solution.py:82
  550.2 61.6 %while.71 = (s32[]{:T(128)}, bf16[8,256,128]{2,1,0:T(8,128)(2,1)}, bf16[8,1536,128]{2,1,0:T(8,128)(2,1)}, bf16[8,256,128]{2,1,0:T(8,128)(2,1)S(1)}, bf16[5,128,1...) while((s32[]{:T(128)}, bf16[8,256,128]{2,1,0:T(8,128)(2,1)}, ...), condition=%wide.region_27.28_spmd, body=%wide.region_22.27_spmd.sunk | while | flops 290131456 | bytes 7891117 | solution.py:86
  (737 shorter events, 276.2 us)
Async XLA Ops:
  0.6 18.8 %copy-start.2 = (bf16[8,256,128]{2,1,0:T(8,128)(2,1)S(1)}, bf16[8,256,128]{2,1,0:T(8,128)(2,1)}, u32[]{:S(2)}) copy-start(bf16[8,256,128]{2,1,0:T(8,128)(2,1)} %param.25) | copy-start | bytes 1572868
  0.6 30.9 %copy-start.12 = (s32[8]{0:T(128)S(1)}, s32[8]{0:T(128)}, u32[]{:S(2)}) copy-start(s32[8]{0:T(128)} %param.33) | copy-start | bytes 100
  1.5 31.2 %copy-start = (s32[8]{0:T(128)S(1)}, s32[8]{0:T(128)}, u32[]{:S(2)}) copy-start(s32[8]{0:T(128)} %param.29) | copy-start | bytes 100
  1.5 41.5 %copy-start.10 = (s32[8,2]{0,1:T(2,128)S(1)}, s32[8,2]{0,1:T(2,128)}, u32[]{:S(2)}) copy-start(s32[8,2]{0,1:T(2,128)} %param.31) | copy-start | bytes 196
  1.5 41.5 %copy-start.5 = (bf16[3,5,128,128]{3,2,1,0:T(8,128)(2,1)S(1)}, bf16[3,5,128,128]{3,2,1,0:T(8,128)(2,1)}, u32[]{:S(2)}) copy-start(bf16[3,5,128,128]{3,2,1,0:T(8,128)(2,1)} %param.34) | copy-start | bytes 1474564
  19.4 23.6 %copy-start.8 = (f32[3,6,128]{2,1,0:T(8,128)S(1)}, f32[3,6,128]{2,1,0:T(8,128)}, u32[]{:S(2)}) copy-start(f32[3,6,128]{2,1,0:T(8,128)} %param.36) | copy-start | bytes 27652
  19.4 55.1 %collective-permute-start = (bf16[8,128,128]{2,1,0:T(8,128)(2,1)}, bf16[8,128,128]{2,1,0:T(8,128)(2,1)}, u32[]{:S(2)}, u32[]{:S(2)}) collective-permute-start(bf16[8,128,128]{2,1,0:T(8,128)(2,1)} %bitcast.82), channel_id=1, source_target_pairs={{0,1},{1,2},{2,3},{3,4},{4,5},{5,6},{6,7},{7,8},{8,9},{9,10},{10,1... | collective-permute-start | bytes 786440 | tf_op jit(solution)/shard_map/ppermute | solution.py:11
  30.0 46.1 %collective-permute-start.1 = (bf16[8,128,128]{2,1,0:T(8,128)(2,1)}, bf16[8,128,128]{2,1,0:T(8,128)(2,1)}, u32[]{:S(2)}, u32[]{:S(2)}) collective-permute-start(bf16[8,128,128]{2,1,0:T(8,128)(2,1)} %bitcast.86), channel_id=1, source_target_pairs={{0,32},{32,64},{64,96},{96,0},{1,33},{33,65},{65,97},{97,1},{2,34}... | collective-permute-start | bytes 786440 | tf_op jit(solution)/shard_map/ppermute | solution.py:11
  34.1 165.9 %all-to-all-start.1 = ((s32[32,1,2]{2,1,0:T(1,128)}), s32[32,1,2]{2,1,0:T(1,128)S(1)}, u32[]{:S(2)}, u32[]{:S(2)}) async-start(s32[32,1,2]{2,1,0:T(1,128)} %copy.72), calls=%async_computation.1 | async-start | bytes 32768 | tf_op jit(solution)/shard_map/all_to_all | solution.py:146
  43.1 3.2 copy-start.3
  43.1 3.2 copy-start.4
  46.3 26.2 %copy-start.9 = (f32[3,2,128]{2,1,0:T(2,128)S(1)}, f32[3,2,128]{2,1,0:T(2,128)}, u32[]{:S(2)}) copy-start(f32[3,2,128]{2,1,0:T(2,128)} %param.37) | copy-start | bytes 9220
  46.3 26.2 %copy-start.7 = (s32[8,2,128]{2,1,0:T(2,128)S(1)}, s32[8,2,128]{2,1,0:T(2,128)}, u32[]{:S(2)}) copy-start(s32[8,2,128]{2,1,0:T(2,128)} %param.30) | copy-start | bytes 24580
  72.5 2.0 copy-start.6
  164.6 31.4 %collective-permute-start.2 = (bf16[8,128,128]{2,1,0:T(8,128)(2,1)}, bf16[8,128,128]{2,1,0:T(8,128)(2,1)}, u32[]{:S(2)}, u32[]{:S(2)}) collective-permute-start(bf16[8,128,128]{2,1,0:T(8,128)(2,1)} %bitcast.92), channel_id=1, source_target_pairs={{0,1},{1,2},{2,3},{3,4},{4,5},{5,6},{6,7},{7,8},{8,9},{9,10},{10,1... | collective-permute-start | bytes 786440 | tf_op jit(solution)/shard_map/ppermute | solution.py:11
  164.7 32.9 %collective-permute-start.3 = (bf16[8,128,128]{2,1,0:T(8,128)(2,1)}, bf16[8,128,128]{2,1,0:T(8,128)(2,1)}, u32[]{:S(2)}, u32[]{:S(2)}) collective-permute-start(bf16[8,128,128]{2,1,0:T(8,128)(2,1)} %bitcast.93), channel_id=1, source_target_pairs={{0,32},{32,64},{64,96},{96,0},{1,33},{33,65},{65,97},{97,1},{2,34}... | collective-permute-start | bytes 786440 | tf_op jit(solution)/shard_map/ppermute | solution.py:11
  200.0 73.7 %all-to-all-start.2 = ((s32[32,1,3328]{2,1,0:T(1,128)}), s32[32,1,3328]{2,1,0:T(1,128)}, u32[]{:S(2)}, u32[]{:S(2)}) async-start(s32[32,1,3328]{2,1,0:T(1,128)} %copy.74), calls=%async_computation.2 | async-start | bytes 851968 | tf_op jit(solution)/shard_map/all_to_all | solution.py:145
  273.7 7.7 %copy-start.1 = (bf16[8,1536,128]{1,2,0:T(8,128)(2,1)S(1)}, bf16[8,1536,128]{1,2,0:T(8,128)(2,1)}, u32[]{:S(2)}) copy-start(bf16[8,1536,128]{1,2,0:T(8,128)(2,1)} %get-tuple-element.352) | copy-start | bytes 9437188
  273.7 32.1 %all-to-all-start = ((bf16[32,256,128]{2,1,0:T(8,128)(2,1)}), bf16[32,256,128]{2,1,0:T(8,128)(2,1)}, u32[]{:S(2)}, u32[]{:S(2)}) async-start(bf16[32,256,128]{2,1,0:T(8,128)(2,1)} %gather_fusion.8), calls=%async_computation | async-start | bytes 4194304 | tf_op jit(solution)/shard_map/all_to_all | solution.py:143
  287.8 27.6 %copy-start.11 = (s32[8,2]{0,1:T(2,128)S(1)}, s32[8,2]{0,1:T(2,128)}, u32[]{:S(2)}) copy-start(s32[8,2]{0,1:T(2,128)} %param.32) | copy-start | bytes 196
  305.9 206.8 %all-to-all-start.3 = ((bf16[32,1536,128]{1,2,0:T(8,128)(2,1)}), bf16[32,1536,128]{1,2,0:T(8,128)(2,1)}, u32[]{:S(2)}, u32[]{:S(2)}) async-start(bf16[32,1536,128]{1,2,0:T(8,128)(2,1)} %gather_fusion.15), calls=%async_computation.3 | async-start | bytes 25165824 | tf_op jit(solution)/shard_map/all_to_all | solution.py:144
  326.1 110.6 %collective-permute-start.4 = (bf16[8,128,128]{2,1,0:T(8,128)(2,1)S(1)}, bf16[8,128,128]{2,1,0:T(8,128)(2,1)S(1)}, u32[]{:S(2)}, u32[]{:S(2)}) collective-permute-start(bf16[8,128,128]{2,1,0:T(8,128)(2,1)S(1)} %bitcast.503), channel_id=1, source_target_pairs={{0,1},{1,2},{2,3},{3,4},{4,5},{5,6},{6,7},{7,8},{8,9},{9,10},{10,1... | collective-permute-start | bytes 786440 | tf_op jit(solution)/shard_map/ppermute | solution.py:11
  332.1 105.2 %collective-permute-start.5 = (bf16[8,128,128]{2,1,0:T(8,128)(2,1)S(1)}, bf16[8,128,128]{2,1,0:T(8,128)(2,1)S(1)}, u32[]{:S(2)}, u32[]{:S(2)}) collective-permute-start(bf16[8,128,128]{2,1,0:T(8,128)(2,1)S(1)} %bitcast.504), channel_id=1, source_target_pairs={{0,32},{32,64},{64,96},{96,0},{1,33},{33,65},{65,97},{97,1},{2,34}... | collective-permute-start | bytes 786440 | tf_op jit(solution)/shard_map/ppermute | solution.py:11
where the time goes:
time: 616 us; the launch traced here: 612 us
  waiting for transfers between devices  196 us (32%)
  matrix products  161 us (26%)
  local copies, waits for them, and re-layouts  152 us (25%)
  other arithmetic  59.4 us (10%)
  starting transfers between devices  39.1 us (6%)
    dot_general x192, matrix products, product(): return jnp.dot(left, right, preferred_element_type=jnp.float32)  161 us
    ppermute x6, waiting for transfers between devices, shifted(): lax.ppermute(shard, axis, [(i, (i + by) % devices) for i in range(devices)])  103 us
    all_to_all x1, waiting for transfers between devices, local(): lax.all_to_all(edge_state[source], 'gy', split_axis=0, concat_axis=0, til...  74.7 us
    gather x3, local copies, waits for them, and re-layouts, fetch_ghosts(): along_gy = vertex_state[patch_rows, border_rows[:, 0]]  34.3 us
    gather x3, local copies, waits for them, and re-layouts, fetch_ghosts(): along_gx = vertex_state[patch_rows, border_rows[:, 1]]  26.9 us
    dynamic_update_slice x24, other arithmetic, run_step(): lax.map(lambda pieces: patch_finish(layer_weights, pieces), (vertex_state...  26.1 us
    all_to_all x1, waiting for transfers between devices, local(): lax.all_to_all(vertex_state[source], 'gy', split_axis=0, concat_axis=0, t...  18 us
    dynamic_update_slice x48, local copies, waits for them, and re-layouts, run_step(): lax.map(lambda pieces: patch_finish(layer_weights, pieces), (vertex_state...  15 us
  transfers between devices with their start and end apart: 10, of which 3 were waited for; matrix products, arithmetic and copies ran while one was open for 42% of the time, Pallas kernels for 0%

commit v1 on v0

v1 whole, which is shorter than its diff:
```python
import jax
import jax.numpy as jnp
from jax import lax
from jax.sharding import PartitionSpec as P
from jax.experimental import pallas as pl
from jax.experimental.pallas import tpu as pltpu

F = 128
V = 256
E = 1536
CH = 256
EPS = 1e-05
f32 = jnp.float32
bf16 = jnp.bfloat16


def mm(a, b):
    return jnp.dot(a, b, preferred_element_type=f32)


def mm_nt(a, b):
    return lax.dot_general(a, b, (((1,), (1,)), ((), ())), preferred_element_type=f32)


def column(row):
    return jnp.broadcast_to(row, (F, F)).T


def flip(w):
    return w.astype(f32).T.astype(bf16)


def sublane_ids(rows):
    return lax.broadcasted_iota(jnp.int32, (rows, CH), 0).astype(f32).astype(bf16)


def one_hot(row, ids):
    return jnp.where(row == ids, jnp.ones((), bf16), jnp.zeros((), bf16))


def border_terms(terms, rows, ids):
    row = jnp.concatenate([rows[0:1], rows[1:2]], axis=1).astype(f32).astype(bf16)
    return mm(terms, one_hot(row, ids)).astype(bf16)


def start_kernel(perm, v_ref, border_ref, wn_ref, gy_ref, gx_ref):
    n = gy_ref.shape[0]
    wsT = flip(wn_ref[0, 0])
    ids = sublane_ids(V)
    for k in range(n):
        terms = mm_nt(wsT, v_ref[perm[k]]).astype(bf16)
        got = border_terms(terms, border_ref[perm[k]], ids)
        gy_ref[k] = got[:, :128]
        gx_ref[k] = got[:, 128:]


def step_kernel(perm, counts, v_ref, e_ref, gy_ref, gx_ref, s_ref, r_ref, border_ref,
                wi_ref, wn_ref, wo_ref, b_ref, g_ref, *rest, n, first, last):
    if last:
        out_ref, scr = rest[0], rest[1:]
    else:
        vo_ref, eo_ref, gyo_ref, gxo_ref = rest[:4]
        scr = rest[4:]
    wrT_s, wsT_s, woT_s, weT_s, cols_s, agg_s = scr
    k = pl.program_id(0)

    @pl.when(k == 0)
    def _():
        weT_s[...] = flip(wi_ref[0, 0])
        wsT_s[...] = flip(wi_ref[0, 1])
        wrT_s[...] = flip(wi_ref[0, 2])
        wo = wo_ref[0, 0].astype(f32)
        woT_s[...] = wo.T.astype(bf16)
        b1 = b_ref[0, 1:2]
        cols_s[0] = column(b_ref[0, 0:1])
        cols_s[1] = column(b1)
        cols_s[2] = column(g_ref[0, 0:1])
        cols_s[3] = column(b_ref[0, 2:3])

    src = perm[k]
    vrow = src if first else k
    v = v_ref[vrow]
    count = counts[src]
    own = mm_nt(wsT_s[...], v).astype(bf16)
    recv = mm_nt(wrT_s[...], v)
    b0 = cols_s[0]
    recv = recv.astype(bf16)
    ghost = jnp.concatenate([gy_ref[k], gx_ref[k]], axis=1)
    lhs_s = jnp.concatenate([own, ghost], axis=0)
    weT = weT_s[...]
    lhs_r = jnp.concatenate([
        jnp.concatenate([weT, recv[:, :128]], axis=1),
        jnp.concatenate([weT, recv[:, 128:]], axis=1)], axis=0)
    woT = woT_s[...]
    ids = sublane_ids(V)
    agg = None
    for c in range(E // CH):
        lo = c * CH
        s = s_ref[pl.ds(src, 1), lo:lo + CH]
        r = r_ref[pl.ds(src, 1), lo:lo + CH]
        live = (lax.broadcasted_iota(jnp.int32, (1, CH), 1) + lo) < count
        s_hi = s >= V
        r_hi = r >= 128
        s_low = jnp.where(s_hi, s - V, s).astype(f32).astype(bf16)
        r_low = jnp.where(r_hi, r - 128, r).astype(f32).astype(bf16)
        oh_s = one_hot(s_low, ids)
        oh_r = one_hot(r_low, ids[:128])
        if first:
            e_b = e_ref[0, lo:lo + CH, :].T
        else:
            e_b = e_ref[0, :, lo:lo + CH]
        e_f = e_b.astype(f32)
        sg = mm(lhs_s, oh_s)
        er = mm(lhs_r, jnp.concatenate([e_b, oh_r], axis=0))
        pre = jnp.where(s_hi, sg[128:], sg[:128]) + jnp.where(r_hi, er[128:], er[:128])
        pre = pre + jnp.concatenate([b0, b0], axis=1)
        h = jnp.maximum(pre, 0.0).astype(bf16)
        b1 = cols_s[1]
        center = mm(woT, h) + jnp.concatenate([b1, b1], axis=1)
        center = center - jnp.sum(center, axis=0, keepdims=True) * (1.0 / F)
        spread = jnp.sum(center * center, axis=0, keepdims=True) * (1.0 / F)
        inv = lax.rsqrt(spread + EPS)
        g, sh = cols_s[2], cols_s[3]
        upd = center * inv * jnp.concatenate([g, g], axis=1) + jnp.concatenate([sh, sh], axis=1)
        fresh = jnp.where(live, e_f + upd, e_f).astype(bf16)
        one = jnp.ones((), f32)
        zero = jnp.zeros((), f32)
        m_lo = jnp.where(jnp.logical_and(live, r < 128), one, zero).astype(bf16)
        m_hi = jnp.where(jnp.logical_and(live, r_hi), one, zero).astype(bf16)
        oh_v = jnp.concatenate([oh_r * m_lo, oh_r * m_hi], axis=0)
        part = mm_nt(oh_v, fresh)
        agg = part if agg is None else agg + part
        if last:
            rows = fresh.T
            for q in range(CH // 16):
                at = lo + q * 16
                out_ref[at // 48, k, at % 48:at % 48 + 16, :] = rows[q * 16:q * 16 + 16]
        else:
            eo_ref[0, :, lo:lo + CH] = fresh
    agg_s[k] = agg.astype(bf16)

    @pl.when(k == n - 1)
    def _():
        if first:
            vs = [v_ref[perm[i]] for i in range(n)]
        else:
            vs = [v_ref[i] for i in range(n)]
        vb = jnp.concatenate(vs, axis=0)
        ab = jnp.concatenate([agg_s[i] for i in range(n)], axis=0)
        wva = jnp.concatenate([wi_ref[0, 3], wi_ref[0, 4]], axis=0)
        hid = mm(jnp.concatenate([vb, ab], axis=1), wva) + b_ref[0, 3:4]
        hid = jnp.maximum(hid, 0.0).astype(bf16)
        center = mm(hid, wo_ref[0, 1]) + b_ref[0, 4:5]
        center = center - jnp.mean(center, axis=1, keepdims=True)
        spread = jnp.mean(center * center, axis=1, keepdims=True)
        upd = center * lax.rsqrt(spread + EPS) * g_ref[0, 1:2] + b_ref[0, 5:6]
        fresh_v = (vb.astype(f32) + upd).astype(bf16)
        if last:
            for i in range(n):
                for q in range(32):
                    at = i * V + q * 8
                    out_ref[q, i, 48:56, :] = fresh_v[at:at + 8]
        else:
            wnT = flip(wn_ref[0, 0])
            terms = mm_nt(wnT, fresh_v).astype(bf16)
            ids2 = sublane_ids(V)
            for i in range(n):
                vo_ref[i] = fresh_v[i * V:(i + 1) * V]
                got = border_terms(terms[:, i * V:(i + 1) * V], border_ref[perm[i]], ids2)
                gyo_ref[i] = got[:, :128]
                gxo_ref[i] = got[:, 128:]


def whole(shape):
    zeros = (0,) * len(shape)
    return pl.BlockSpec(tuple(shape), lambda *_: zeros)


def start_call(n, perm, v, border, w_in, interpret=False):
    return pl.pallas_call(
        start_kernel,
        grid_spec=pltpu.PrefetchScalarGridSpec(
            num_scalar_prefetch=1, grid=(1,),
            in_specs=[whole(v.shape), whole(border.shape),
                      pl.BlockSpec((1, 1, F, F), lambda *_: (0, 1, 0, 0))],
            out_specs=[whole((n, F, 128)), whole((n, F, 128))]),
        out_shape=[jax.ShapeDtypeStruct((n, F, 128), bf16)] * 2,
        interpret=interpret, name="start",
    )(perm, v, border, w_in)


def step_call(step, n, perm, counts, v, e, gy, gx, s, r, border, w_in, w_out, biases, gains,
              *, first, last, interpret=False):
    import functools
    nxt = min(step + 1, 2)
    if first:
        e_spec = pl.BlockSpec((1, E, F), lambda k, p, c: (p[k], 0, 0))
    else:
        e_spec = pl.BlockSpec((1, F, E), lambda k, p, c: (k, 0, 0))
    if last:
        out_specs = [whole((32, n, 56, F))]
        out_shape = [jax.ShapeDtypeStruct((32, n, 56, F), bf16)]
    else:
        out_specs = [whole((n, V, F)), pl.BlockSpec((1, F, E), lambda k, p, c: (k, 0, 0)),
                     whole((n, F, 128)), whole((n, F, 128))]
        out_shape = [jax.ShapeDtypeStruct((n, V, F), bf16), jax.ShapeDtypeStruct((n, F, E), bf16),
                     jax.ShapeDtypeStruct((n, F, 128), bf16), jax.ShapeDtypeStruct((n, F, 128), bf16)]
    return pl.pallas_call(
        functools.partial(step_kernel, n=n, first=first, last=last),
        grid_spec=pltpu.PrefetchScalarGridSpec(
            num_scalar_prefetch=2, grid=(n,),
            in_specs=[whole(v.shape), e_spec, whole(gy.shape), whole(gx.shape),
                      whole(s.shape), whole(r.shape), whole(border.shape),
                      pl.BlockSpec((1, 5, F, F), lambda *_: (step, 0, 0, 0)),
                      pl.BlockSpec((1, 1, F, F), lambda *_: (nxt, 1, 0, 0)),
                      pl.BlockSpec((1, 2, F, F), lambda *_: (step, 0, 0, 0)),
                      pl.BlockSpec((1, 6, F), lambda *_: (step, 0, 0)),
                      pl.BlockSpec((1, 2, F), lambda *_: (step, 0, 0))],
            out_specs=out_specs,
            scratch_shapes=[pltpu.VMEM((F, F), bf16)] * 4 + [
                pltpu.VMEM((4, F, F), f32), pltpu.VMEM((n, V, F), bf16)]),
        out_shape=out_shape,
        interpret=interpret, name=f"step{step}",
    )(perm, counts, v, e, gy, gx, s, r, border, w_in, w_in, w_out, biases, gains)


def roll_kernel(shifts, in_ref, out_ref):
    d = shifts[pl.program_id(0)]

    def body(j, carry):
        at = j + d
        at = jnp.where(at >= 32, at - 32, at)
        out_ref[at, 0] = in_ref[j, 0]
        return carry

    lax.fori_loop(0, 32, body, 0, unroll=4)


def roll_call(shifts, got):
    block = pl.BlockSpec((32, 1, 56, F), lambda k, d: (0, k, 0, 0))
    return pl.pallas_call(
        roll_kernel,
        grid_spec=pltpu.PrefetchScalarGridSpec(
            num_scalar_prefetch=1, grid=(got.shape[1],), in_specs=[block], out_specs=block),
        out_shape=jax.ShapeDtypeStruct(got.shape, bf16), name="roll",
    )(shifts, got)


def place_kernel(slots, in_ref, v_ref, e_ref):
    for q in range(32):
        e_ref[0, q * 48:q * 48 + 48, :] = in_ref[q, 0, :48, :]
        v_ref[0, q * 8:q * 8 + 8, :] = in_ref[q, 0, 48:, :]


def place_call(slots, got):
    n = got.shape[1]
    return pl.pallas_call(
        place_kernel,
        grid_spec=pltpu.PrefetchScalarGridSpec(
            num_scalar_prefetch=1, grid=(n,),
            in_specs=[pl.BlockSpec((32, 1, 56, F), lambda k, d: (0, k, 0, 0))],
            out_specs=[pl.BlockSpec((1, V, F), lambda k, d: (d[k], 0, 0)),
                       pl.BlockSpec((1, E, F), lambda k, d: (d[k], 0, 0))]),
        out_shape=[jax.ShapeDtypeStruct((n, V, F), bf16), jax.ShapeDtypeStruct((n, E, F), bf16)],
        name="place",
    )(slots, got)


def shifted(shard, axis):
    devices = lax.axis_size(axis)
    return lax.ppermute(shard, axis, [(i, (i + 1) % devices) for i in range(devices)])


def exchange(gy, gx):
    return shifted(gy, "gy"), shifted(gx, "gx")


def spread(values):
    return lax.all_to_all(values, "gy", split_axis=0, concat_axis=0, tiled=True)


def local(vertex_state, edge_state, senders, receivers, counts, border_rows, old_neighbours,
          new_neighbours, new_place, weights_in, weights_out, biases, norm_gains):
    n = vertex_state.shape[0]
    cycle = lax.axis_size("gy")
    me = lax.axis_index("gy")
    moved = ((new_place // n) % cycle - me) % cycle
    slots = jnp.arange(n, dtype=jnp.int32)
    order = moved * n + slots
    rank = jnp.sum((order[None, :] < order[:, None]).astype(jnp.int32), axis=1)
    chosen = (rank[None, :] == slots[:, None]).astype(jnp.int32)
    perm = jnp.sum(chosen * slots[None, :], axis=1)
    shifts = jnp.sum(chosen * moved[None, :], axis=1)
    landing = jnp.sum(chosen * (new_place % n)[None, :], axis=1)
    devices = jnp.arange(cycle, dtype=jnp.int32)
    goes = ((me + shifts) % cycle)[None, :] == devices[:, None]
    header = spread(jnp.sum(jnp.where(goes, landing[None, :], 0), axis=1))
    comes = ((me - shifts) % cycle)[:, None] == devices[None, :]
    landing = jnp.clip(jnp.sum(jnp.where(comes, header[None, :], 0), axis=1), 0, n - 1)

    rest = (senders, receivers, border_rows, weights_in, weights_out, biases, norm_gains)
    gy, gx = exchange(*start_call(n, perm, vertex_state, border_rows, weights_in))
    v, e, gy, gx = step_call(0, n, perm, counts, vertex_state, edge_state, gy, gx, *rest,
                             first=True, last=False)
    gy, gx = exchange(gy, gx)
    v, e, gy, gx = step_call(1, n, perm, counts, v, e, gy, gx, *rest, first=False, last=False)
    gy, gx = exchange(gy, gx)
    packed, = step_call(2, n, perm, counts, v, e, gy, gx, *rest, first=False, last=True)
    packed = spread(roll_call(shifts, spread(packed)))
    return tuple(place_call(landing, packed))


def solution(mesh):
    along = ("gx", "gy")
    placed = (P(along, None, None), P(along, None, None), P(along, None), P(along, None), P(along),
              P(along, None, None), P(along, None), P(along, None), P(along), P(), P(), P(), P())
    return jax.shard_map(
        local, mesh=mesh, in_specs=placed,
        out_specs=(P(along, None, None), P(along, None, None)), check_vma=False)
```

time: 616 us -> 245 us (0.40)
  the two profiles are of different devices: /device:TPU:36 before, /device:TPU:1 now
where the time goes in v1:
time: 245 us; the launch traced here: 244 us
  waiting for transfers between devices  115 us (47%)
  Pallas kernels  94 us (38%)
  starting transfers between devices  28.9 us (12%)
  other arithmetic  3 us (1%)
  local copies, waits for them, and re-layouts  2.8 us (1%)
    all_to_all x3, waiting for transfers between devices, spread(): return lax.all_to_all(values, 'gy', split_axis=0, concat_axis=0, tiled=True)  89.2 us
    pallas_call x3, Pallas kernels, step_call(): pl.pallas_call(functools.partial(step_kernel, n=n, first=first, last=last...  76.5 us
    ppermute x6, waiting for transfers between devices, shifted(): lax.ppermute(shard, axis, [(i, (i + 1) % devices) for i in range(devices)])  25.6 us
    all_to_all x3, starting transfers between devices, spread(): return lax.all_to_all(values, 'gy', split_axis=0, concat_axis=0, tiled=True)  21.6 us
    pallas_call x1, Pallas kernels, roll_call(): pl.pallas_call(roll_kernel, grid_spec=pltpu.PrefetchScalarGridSpec(num_sc...  7.37 us
    ppermute x6, starting transfers between devices, shifted(): lax.ppermute(shard, axis, [(i, (i + 1) % devices) for i in range(devices)])  7.34 us
    pallas_call x1, Pallas kernels, place_call(): pl.pallas_call(place_kernel, grid_spec=pltpu.PrefetchScalarGridSpec(num_s...  7.07 us
  transfers between devices with their start and end apart: 9, of which 8 were waited for; matrix products, arithmetic and copies ran while one was open for 1% of the time, Pallas kernels for 3%

profile of v1, /device:TPU:1, one launch (start us, length us, event | category | flops | bytes accessed | tf_op | source)
XLA Modules:
  0.0 244.3 jit_solution(599126455865359923)
XLA Ops:
  0.6 0.7 iota_add_fusion
  1.3 0.2 convert_reduce_fusion
  1.5 0.6 select_reduce_fusion
  2.1 3.1 %start.1 = (bf16[8,128,128]{2,1,0:T(8,128)(2,1)}, bf16[8,128,128]{2,1,0:T(8,128)(2,1)}) custom-call(s32[8]{0:T(128)} %get-tuple-element.22.perm, bf16[8,256,128]{2,1,0:T(8,128)(2,1)} %v_ref.3, s32[8,2,128]{2,1,0:T(2,128)} %border_ref.7, bf16[3,5,128,128]{3,2,1,0:T(8,128)(2,1)} %wn_ref.7), custom_call_target="tpu_custom_call" | custom-call | tf_op jit(solution)/shard_map/start/pallas_call | solution.py:180
  5.2 3.0 %collective-permute-start = (bf16[8,128,128]{2,1,0:T(8,128)(2,1)}, bf16[8,128,128]{2,1,0:T(8,128)(2,1)S(1)}, u32[]{:S(2)}, u32[]{:S(2)}) collective-permute-start(bf16[8,128,128]{2,1,0:T(8,128)(2,1)} %get-tuple-element.12), channel_id=1, source_target_pairs={{0,1},{1,2},{2,3},{3,4},{4,5},{5,6},{6,7},{7,8},{8,9},{9,10},{10,1... | collective-permute-start | bytes 786440 | tf_op jit(solution)/shard_map/ppermute | solution.py:271
  8.3 1.3 collective-permute-start.1
  9.5 2.3 collective-permute-done.gy_ref
  11.9 4.6 %collective-permute-done.1.gx_ref = bf16[8,128,128]{2,1,0:T(8,128)(2,1)S(1)} collective-permute-done((bf16[8,128,128]{2,1,0:T(8,128)(2,1)}, bf16[8,128,128]{2,1,0:T(8,128)(2,1)S(1)}, u32[]{:S(2)}, u32[]{:S(2)}) %collective-permute-start.1) | collective-permute-done | bytes 262176 | tf_op jit(solution)/shard_map/ppermute | solution.py:271
  16.5 0.7 copy-done.3
  17.2 25.4 %step0.1 = (bf16[8,256,128]{2,1,0:T(8,128)(2,1)}, bf16[8,128,1536]{2,1,0:T(8,128)(2,1)}, bf16[8,128,128]{2,1,0:T(8,128)(2,1)}, bf16[8,128,128]{2,1,0:T(8,128)(2,1)}) custom-call(s32[8]{0:T(128)} %get-tuple-element.22.perm, s32[8]{0:T(128)} %counts.5, bf16[8,256,128]{2,1,0:T(8,128)(2,1)} %v_ref.3, bf16[8,1536,128]{2,1,0:T(8,128)(2,1)} %e_ref.1, ...), custom_call_target="tpu_custom_call" | custom-call | tf_op jit(solution)/shard_map/step0/pallas_call | solution.py:208
  42.7 1.3 collective-permute-start.2
  43.9 0.2 collective-permute-start.3
  44.1 3.5 %collective-permute-done.2.gy_ref = bf16[8,128,128]{2,1,0:T(8,128)(2,1)S(1)} collective-permute-done((bf16[8,128,128]{2,1,0:T(8,128)(2,1)}, bf16[8,128,128]{2,1,0:T(8,128)(2,1)S(1)}, u32[]{:S(2)}, u32[]{:S(2)}) %collective-permute-start.2) | collective-permute-done | bytes 262176 | tf_op jit(solution)/shard_map/ppermute | solution.py:271
  47.5 5.9 %collective-permute-done.3.gx_ref = bf16[8,128,128]{2,1,0:T(8,128)(2,1)S(1)} collective-permute-done((bf16[8,128,128]{2,1,0:T(8,128)(2,1)}, bf16[8,128,128]{2,1,0:T(8,128)(2,1)S(1)}, u32[]{:S(2)}, u32[]{:S(2)}) %collective-permute-start.3) | collective-permute-done | bytes 262176 | tf_op jit(solution)/shard_map/ppermute | solution.py:271
  53.5 0.7 copy-done.2
  54.2 25.3 %step1.1 = (bf16[8,256,128]{2,1,0:T(8,128)(2,1)}, bf16[8,128,1536]{2,1,0:T(8,128)(2,1)}, bf16[8,128,128]{2,1,0:T(8,128)(2,1)}, bf16[8,128,128]{2,1,0:T(8,128)(2,1)}) custom-call(s32[8]{0:T(128)} %get-tuple-element.22.perm, s32[8]{0:T(128)} %counts.5, bf16[8,256,128]{2,1,0:T(8,128)(2,1)} %get-tuple-element.14.v_ref, ...), custom_call_target="tpu_custom_call" | custom-call | tf_op jit(solution)/shard_map/step1/pallas_call | solution.py:208
  79.5 1.6 collective-permute-start.4
  81.1 3.6 %collective-permute-done.4.gy_ref = bf16[8,128,128]{2,1,0:T(8,128)(2,1)S(1)} collective-permute-done((bf16[8,128,128]{2,1,0:T(8,128)(2,1)}, bf16[8,128,128]{2,1,0:T(8,128)(2,1)S(1)}, u32[]{:S(2)}, u32[]{:S(2)}) %collective-permute-start.4) | collective-permute-done | bytes 262176 | tf_op jit(solution)/shard_map/ppermute | solution.py:271
  84.8 5.6 %collective-permute-done.5.gx_ref = bf16[8,128,128]{2,1,0:T(8,128)(2,1)S(1)} collective-permute-done((bf16[8,128,128]{2,1,0:T(8,128)(2,1)}, bf16[8,128,128]{2,1,0:T(8,128)(2,1)S(1)}, u32[]{:S(2)}, u32[]{:S(2)}) %collective-permute-start.5) | collective-permute-done | bytes 262176 | tf_op jit(solution)/shard_map/ppermute | solution.py:271
  90.4 0.7 copy-done.5
  91.1 25.7 %step2.1 = bf16[32,8,56,128]{3,2,1,0:T(8,128)(2,1)} custom-call(s32[8]{0:T(128)} %get-tuple-element.22.perm, s32[8]{0:T(128)} %counts.5, bf16[8,256,128]{2,1,0:T(8,128)(2,1)} %get-tuple-element.18.v_ref, bf16[8,128,1536]{2,1,0:T(8,128)(2,1)} %get-tuple-element.19.e_ref, bf16[8,128,128]{2,1,0:T(8,128)(2,1)} %copy-done.4, bf16[8,128,128]{2,1,0:T(8,128)(2,1)} %copy-done.5, ...), custom_call_target="tpu_custom_call" | custom-call | tf_op jit(solution)/shard_map/step2/pallas_call | solution.py:208
  116.8 7.5 %all-to-all-start.1 = ((bf16[32,8,56,128]{3,2,1,0:T(8,128)(2,1)}), bf16[32,8,56,128]{3,2,1,0:T(8,128)(2,1)}, u32[]{:S(2)}, u32[]{:S(2)}) async-start(bf16[32,8,56,128]{3,2,1,0:T(8,128)(2,1)} %step2.1), calls=%async_computation.1 | async-start | bytes 7340032 | tf_op jit(solution)/shard_map/all_to_all | solution.py:279
  124.4 0.7 copy.15
  125.1 44.9 %all-to-all-done.1.in_ref = bf16[32,8,56,128]{3,2,1,0:T(8,128)(2,1)} async-done(((bf16[32,8,56,128]{3,2,1,0:T(8,128)(2,1)}), bf16[32,8,56,128]{3,2,1,0:T(8,128)(2,1)}, u32[]{:S(2)}, u32[]{:S(2)}) %all-to-all-start.1) | async-done | bytes 3670048 | tf_op jit(solution)/shard_map/all_to_all | solution.py:279
  170.0 6.7 %all-to-all-start = ((s32[32,1,1]{2,1,0:T(1,128)}), s32[32,1,1]{2,1,0:T(1,128)S(1)}, u32[]{:S(2)}, u32[]{:S(2)}) async-start(s32[32,1,1]{2,1,0:T(1,128)} %copy.15), calls=%async_computation | async-start | bytes 32768 | tf_op jit(solution)/shard_map/all_to_all | solution.py:279
  176.7 7.4 %roll.1 = bf16[32,8,56,128]{3,2,1,0:T(8,128)(2,1)} custom-call(s32[8]{0:T(128)} %copy-done.6, bf16[32,8,56,128]{3,2,1,0:T(8,128)(2,1)} %all-to-all-done.1.in_ref), custom_call_target="tpu_custom_call" | custom-call | tf_op jit(solution)/shard_map/roll/pallas_call | solution.py:241
  184.1 7.4 %all-to-all-start.2 = ((bf16[32,8,56,128]{3,2,1,0:T(8,128)(2,1)}), bf16[32,8,56,128]{3,2,1,0:T(8,128)(2,1)}, u32[]{:S(2)}, u32[]{:S(2)}) async-start(bf16[32,8,56,128]{3,2,1,0:T(8,128)(2,1)} %roll.1), calls=%async_computation.2 | async-start | bytes 7340032 | tf_op jit(solution)/shard_map/all_to_all | solution.py:279
  191.5 0.7 reduce
  192.2 0.2 select_reduce_fusion.1
  192.3 0.6 broadcast_clamp_fusion.slots
  192.9 44.3 %all-to-all-done.2.in_ref = bf16[32,8,56,128]{3,2,1,0:T(8,128)(2,1)} async-done(((bf16[32,8,56,128]{3,2,1,0:T(8,128)(2,1)}), bf16[32,8,56,128]{3,2,1,0:T(8,128)(2,1)}, u32[]{:S(2)}, u32[]{:S(2)}) %all-to-all-start.2) | async-done | bytes 3670048 | tf_op jit(solution)/shard_map/all_to_all | solution.py:279
  237.2 7.1 %place.1 = (bf16[8,256,128]{2,1,0:T(8,128)(2,1)}, bf16[8,1536,128]{2,1,0:T(8,128)(2,1)}) custom-call(s32[8]{0:T(128)} %broadcast_clamp_fusion.slots, bf16[32,8,56,128]{3,2,1,0:T(8,128)(2,1)} %all-to-all-done.2.in_ref), custom_call_target="tpu_custom_call" | custom-call | tf_op jit(solution)/shard_map/place/pallas_call | solution.py:257
  (15 shorter events, 0.1 us)
Async XLA Ops:
  2.1 122.1 %copy-start.6 = (s32[8]{0:T(128)}, s32[8]{0:T(128)S(1)}, u32[]{:S(2)}) copy-start(s32[8]{0:T(128)S(1)} %get-tuple-element.24.shifts) | copy-start | bytes 100
  5.2 6.6 %collective-permute-start = (bf16[8,128,128]{2,1,0:T(8,128)(2,1)}, bf16[8,128,128]{2,1,0:T(8,128)(2,1)S(1)}, u32[]{:S(2)}, u32[]{:S(2)}) collective-permute-start(bf16[8,128,128]{2,1,0:T(8,128)(2,1)} %get-tuple-element.12), channel_id=1, source_target_pairs={{0,1},{1,2},{2,3},{3,4},{4,5},{5,6},{6,7},{7,8},{8,9},{9,10},{10,1... | collective-permute-start | bytes 786440 | tf_op jit(solution)/shard_map/ppermute | solution.py:271
  8.3 8.3 %collective-permute-start.1 = (bf16[8,128,128]{2,1,0:T(8,128)(2,1)}, bf16[8,128,128]{2,1,0:T(8,128)(2,1)S(1)}, u32[]{:S(2)}, u32[]{:S(2)}) collective-permute-start(bf16[8,128,128]{2,1,0:T(8,128)(2,1)} %get-tuple-element.13), channel_id=1, source_target_pairs={{0,32},{32,64},{64,96},{96,0},{1,33},{33,65},{65,97},{97,1},{2,34}... | collective-permute-start | bytes 786440 | tf_op jit(solution)/shard_map/ppermute | solution.py:271
  11.9 4.7 %copy-start.1 = (bf16[8,128,128]{2,1,0:T(8,128)(2,1)}, bf16[8,128,128]{2,1,0:T(8,128)(2,1)S(1)}, u32[]{:S(2)}) copy-start(bf16[8,128,128]{2,1,0:T(8,128)(2,1)S(1)} %collective-permute-done.gy_ref) | copy-start | bytes 786436
  16.5 0.7 copy-start.3
  42.7 4.9 %collective-permute-start.2 = (bf16[8,128,128]{2,1,0:T(8,128)(2,1)}, bf16[8,128,128]{2,1,0:T(8,128)(2,1)S(1)}, u32[]{:S(2)}, u32[]{:S(2)}) collective-permute-start(bf16[8,128,128]{2,1,0:T(8,128)(2,1)} %get-tuple-element.16), channel_id=1, source_target_pairs={{0,1},{1,2},{2,3},{3,4},{4,5},{5,6},{6,7},{7,8},{8,9},{9,10},{10,1... | collective-permute-start | bytes 786440 | tf_op jit(solution)/shard_map/ppermute | solution.py:271
  43.9 9.6 %collective-permute-start.3 = (bf16[8,128,128]{2,1,0:T(8,128)(2,1)}, bf16[8,128,128]{2,1,0:T(8,128)(2,1)S(1)}, u32[]{:S(2)}, u32[]{:S(2)}) collective-permute-start(bf16[8,128,128]{2,1,0:T(8,128)(2,1)} %get-tuple-element.17), channel_id=1, source_target_pairs={{0,32},{32,64},{64,96},{96,0},{1,33},{33,65},{65,97},{97,1},{2,34}... | collective-permute-start | bytes 786440 | tf_op jit(solution)/shard_map/ppermute | solution.py:271
  47.5 5.9 %copy-start = (bf16[8,128,128]{2,1,0:T(8,128)(2,1)}, bf16[8,128,128]{2,1,0:T(8,128)(2,1)S(1)}, u32[]{:S(2)}) copy-start(bf16[8,128,128]{2,1,0:T(8,128)(2,1)S(1)} %collective-permute-done.2.gy_ref) | copy-start | bytes 786436
  53.5 0.7 copy-start.2
  79.5 5.2 %collective-permute-start.4 = (bf16[8,128,128]{2,1,0:T(8,128)(2,1)}, bf16[8,128,128]{2,1,0:T(8,128)(2,1)S(1)}, u32[]{:S(2)}, u32[]{:S(2)}) collective-permute-start(bf16[8,128,128]{2,1,0:T(8,128)(2,1)} %get-tuple-element.20), channel_id=1, source_target_pairs={{0,1},{1,2},{2,3},{3,4},{4,5},{5,6},{6,7},{7,8},{8,9},{9,10},{10,1... | collective-permute-start | bytes 786440 | tf_op jit(solution)/shard_map/ppermute | solution.py:271
  81.1 9.2 %collective-permute-start.5 = (bf16[8,128,128]{2,1,0:T(8,128)(2,1)}, bf16[8,128,128]{2,1,0:T(8,128)(2,1)S(1)}, u32[]{:S(2)}, u32[]{:S(2)}) collective-permute-start(bf16[8,128,128]{2,1,0:T(8,128)(2,1)} %get-tuple-element.21), channel_id=1, source_target_pairs={{0,32},{32,64},{64,96},{96,0},{1,33},{33,65},{65,97},{97,1},{2,34}... | collective-permute-start | bytes 786440 | tf_op jit(solution)/shard_map/ppermute | solution.py:271
  84.8 5.6 %copy-start.4 = (bf16[8,128,128]{2,1,0:T(8,128)(2,1)}, bf16[8,128,128]{2,1,0:T(8,128)(2,1)S(1)}, u32[]{:S(2)}) copy-start(bf16[8,128,128]{2,1,0:T(8,128)(2,1)S(1)} %collective-permute-done.4.gy_ref) | copy-start | bytes 786436
  90.4 0.7 copy-start.5
  116.8 53.2 %all-to-all-start.1 = ((bf16[32,8,56,128]{3,2,1,0:T(8,128)(2,1)}), bf16[32,8,56,128]{3,2,1,0:T(8,128)(2,1)}, u32[]{:S(2)}, u32[]{:S(2)}) async-start(bf16[32,8,56,128]{3,2,1,0:T(8,128)(2,1)} %step2.1), calls=%async_computation.1 | async-start | bytes 7340032 | tf_op jit(solution)/shard_map/all_to_all | solution.py:279
  170.0 14.1 %all-to-all-start = ((s32[32,1,1]{2,1,0:T(1,128)}), s32[32,1,1]{2,1,0:T(1,128)S(1)}, u32[]{:S(2)}, u32[]{:S(2)}) async-start(s32[32,1,1]{2,1,0:T(1,128)} %copy.15), calls=%async_computation | async-start | bytes 32768 | tf_op jit(solution)/shard_map/all_to_all | solution.py:279
  184.1 53.1 %all-to-all-start.2 = ((bf16[32,8,56,128]{3,2,1,0:T(8,128)(2,1)}), bf16[32,8,56,128]{3,2,1,0:T(8,128)(2,1)}, u32[]{:S(2)}, u32[]{:S(2)}) async-start(bf16[32,8,56,128]{3,2,1,0:T(8,128)(2,1)} %roll.1), calls=%async_computation.2 | async-start | bytes 7340032 | tf_op jit(solution)/shard_map/all_to_all | solution.py:279
